TPU v7x, 128 devices: a whole 4x4x4 slice. The times are simulated.
128 devices in a mesh: batch: 1, src: 16 (over z, y), graph: 8 (over x, core).
Axes of the slice: x: 4, y: 4, z: 4, core: 2. Of those that a mesh axis runs over, the one named last changes fastest.
Arguments:
- adj: bfloat16 [9216, 9216], P(('batch', 'graph'))
- sources: int32 [4096], P(('batch', 'src'))
- level_weight: float32 [2], replicated
Outputs:
- output: float32 [9216], P(('batch', 'graph'))
All inputs are finite; a program needn't handle non-finite values.
Results may differ from a plain program's by a relative error of at most 0.001.
Values are sent between devices in bfloat16 or wider.
A program may use at most 1 GiB of HBM per device.

v0:
```python
import jax
import jax.numpy as jnp
from jax import lax
from jax.sharding import PartitionSpec as P

exact_precision = lax.Precision.HIGHEST


def solution(mesh):
    src_devices = mesh.shape["src"]

    def device_program(adj_slab, src_local, level_weight):
        slab_rows, vertex_count = adj_slab.shape
        src_count = src_local.shape[0]
        levels = level_weight.shape[0] + 1
        row_start = lax.axis_index("graph") * slab_rows
        vertex_ids = row_start + lax.broadcasted_iota(jnp.int32, (slab_rows, 1), 0)
        sigma = jnp.where(vertex_ids == src_local[None, :], 1.0, 0.0).astype(jnp.float32)
        seen = sigma
        sigmas = []
        for level in range(levels):
            partial_counts = jnp.einsum("uv,us->vs", adj_slab, sigma, preferred_element_type=jnp.float32, precision=exact_precision)
            summed = lax.psum_scatter(partial_counts, "graph", scatter_dimension=0, tiled=True)
            sigma = summed * (1.0 - seen)
            seen = jnp.maximum(seen, jnp.where(sigma > 0, 1.0, 0.0))
            sigmas.append(sigma)
        delta = jnp.zeros_like(sigma)
        total = jnp.zeros_like(sigma)
        for level in range(levels - 1, 0, -1):
            sig_upper = sigmas[level]
            reached = sig_upper > 0
            weights = jnp.where(reached, (level_weight[level - 1] + delta) / jnp.where(reached, sig_upper, 1.0), 0.0)
            gathered = lax.all_gather(weights, "graph", axis=0, tiled=True)
            pulled = jnp.einsum("uv,vs->us", adj_slab, gathered, preferred_element_type=jnp.float32, precision=exact_precision)
            delta = sigmas[level - 1] * pulled
            total = total + delta
        scale = vertex_count / (src_count * src_devices * levels ** 3)
        return lax.psum(jnp.sum(total, axis=1) * scale, "src")

    return jax.shard_map(device_program, mesh=mesh,
                         in_specs=(P(("batch", "graph"), None), P(("batch", "src")), P(None)),
                         out_specs=P(("batch", "graph")), check_vma=False)
```

profile of v0, /device:TPU:1, one launch (start us, length us, event | category | flops | bytes accessed | tf_op | source)
XLA Modules:
  0.0 456.6 jit_solution(13825890713338733305)
XLA Ops:
  6.5 0.0 reduce-scatter.4.cloned.1.call-start
  6.5 23.5 %convolution_bitcast_fusion.2 = f32[9216,256]{0,1:T(8,128)} fusion(bf16[1152,9216]{1,0:T(8,128)(2,1)} %param.3, s32[1152]{0:T(1024)S(1)} %iota_add_fusion, s32[256]{0:T(256)} %param.4), kind=kOutput, calls=%fused_computation.2 | convolution fusion | flops 32615497728 | bytes 30676480 | tf_op jit(solution)/shard_map/uv,us->vs/dot_general | solution.py:22
  30.1 0.0 copy-start.2
  30.1 0.0 reduce-scatter.4.cloned.1.call-update
  30.1 0.0 reduce-scatter.6.cloned.1.call-start
  30.2 60.3 %reduce-scatter.4.cloned.1.call-done = f32[1152,256]{0,1:T(8,128)} async-done(((f32[9216,256]{0,1:T(8,128)}), f32[1152,256]{0,1:T(8,128)}) %reduce-scatter.4.cloned.1.call-update) | async-done | bytes 1179664 | tf_op jit(solution)/shard_map/reduce_scatter | solution.py:23
  90.5 0.0 copy-done.2
  90.5 24.4 %convolution_bitcast_fusion.1 = f32[9216,256]{0,1:T(8,128)} fusion(bf16[1152,9216]{1,0:T(8,128)(2,1)} %param.3, f32[1152,256]{0,1:T(8,128)} %reduce-scatter.4.cloned.1.call-done, s32[1152]{0:T(1024)S(1)} %iota_add_fusion, s32[256]{0:T(256)S(1)} %copy-done.2), kind=kOutput, calls=%fused_computation.1 | convolution fusion | flops 32616087552 | bytes 31856128 | tf_op jit(solution)/shard_map/uv,us->vs/dot_general | solution.py:22
  114.9 0.0 copy-start
  114.9 0.0 reduce-scatter.6.cloned.1.call-update
  114.9 0.2 reduce-scatter.8.cloned.1.call-start
  115.1 1.0 copy-done
  116.1 0.4 fusion.11
  116.5 55.7 %reduce-scatter.6.cloned.1.call-done = f32[1152,256]{0,1:T(8,128)} async-done(((f32[9216,256]{0,1:T(8,128)}), f32[1152,256]{0,1:T(8,128)}) %reduce-scatter.6.cloned.1.call-update) | async-done | bytes 1179664 | tf_op jit(solution)/shard_map/reduce_scatter | solution.py:23
  172.2 24.9 %convolution_bitcast_fusion = f32[9216,256]{0,1:T(8,128)} fusion(bf16[1152,9216]{1,0:T(8,128)(2,1)} %param.3, f32[1152,256]{0,1:T(8,128)} %reduce-scatter.6.cloned.1.call-done, pred[1152,256]{0,1:T(32,128)(4,1)S(1)} %fusion.11, s32[1152]{0:T(1024)S(1)} %iota_add_fusion, s32[256]{0:T(256)S(1)} %copy-done.2), kind=kOutput, calls=%fused_computation | convolution fusion | flops 32616677376 | bytes 32151040 | tf_op jit(solution)/shard_map/uv,us->vs/dot_general | solution.py:22
  197.1 0.0 copy-start.3
  197.1 0.0 reduce-scatter.8.cloned.1.call-update
  197.1 0.0 all-gather.3.cloned.1.call-start
  197.1 0.6 copy-done.3
  197.7 0.6 fusion.25
  198.4 56.0 %reduce-scatter.8.cloned.1.call-done = f32[1152,256]{0,1:T(8,128)} async-done(((f32[9216,256]{0,1:T(8,128)}), f32[1152,256]{0,1:T(8,128)}) %reduce-scatter.8.cloned.1.call-update) | async-done | bytes 1179664 | tf_op jit(solution)/shard_map/reduce_scatter | solution.py:23
  254.4 0.0 copy-done.1
  254.4 3.7 compare_select_fusion
  258.1 0.0 all-gather.3.cloned.1.call-update
  258.1 0.3 all-gather.5.cloned.1.call-start
  258.4 54.4 %all-gather.3.cloned.1.call-done = f32[9216,256]{0,1:T(8,128)} async-done(((f32[1152,256]{0,1:T(8,128)}), f32[9216,256]{0,1:T(8,128)}) %all-gather.3.cloned.1.call-update) | async-done | bytes 9437200 | tf_op jit(solution)/shard_map/all_gather | solution.py:33
  312.8 25.4 %divide_select_fusion = (f32[1152,256]{0,1:T(8,128)}, f32[1152,256]{0,1:T(8,128)}) fusion(f32[]{:T(128)} %bitcast.5, f32[1152,256]{0,1:T(8,128)S(1)} %copy-done.1, pred[1152,256]{0,1:T(32,128)(4,1)S(1)} %fusion.11, s32[256]{0:T(256)S(1)} %copy-done.2, s32[1152]{0:T(1024)S(1)} %iota_add_fusion, f32[9216,256]{0,1:T(8,128)} %all-gather.3.cloned.1.call-done, ...), kind=kOutput, calls=%fused_computation.17 | convolution fusion | flops 32618446848 | bytes 34510340 | tf_op jit(solution)/shard_map/uv,vs->us/dot_general | solution.py:34
  338.2 0.0 all-gather.5.cloned.1.call-update
  338.2 54.4 %all-gather.5.cloned.1.call-done = f32[9216,256]{0,1:T(8,128)} async-done(((f32[1152,256]{0,1:T(8,128)}), f32[9216,256]{0,1:T(8,128)}) %all-gather.5.cloned.1.call-update) | async-done | bytes 9437200 | tf_op jit(solution)/shard_map/all_gather | solution.py:33
  392.6 0.0 copy-done.4
  392.6 23.0 %fusion.5 = f32[1152]{0:T(1024)S(1)} fusion(f32[1152,256]{0,1:T(8,128)S(1)} %copy-done.4, f32[9216,256]{0,1:T(8,128)} %all-gather.5.cloned.1.call-done, bf16[1152,9216]{1,0:T(8,128)(2,1)} %param.3, f32[1152,256]{0,1:T(8,128)S(1)} %copy-done, s32[1152]{0:T(1024)S(1)} %iota_add_fusion, s32[256]{0:T(256)S(1)} %copy-done.2), kind=kOutput, calls=%fused_computation.14 | convolution fusion | flops 32616972288 | bytes 33040384 | tf_op jit(solution)/shard_map/uv,vs->us/dot_general | solution.py:34
  415.6 34.5 %psum.7 = f32[1152]{0:T(1024)} all-reduce(f32[1152]{0:T(1024)S(1)} %broadcast_multiply_fusion), channel_id=1, replica_groups=mesh['batch'=1,'src'=16,'graph'=8] {'src'}, use_global_device_ids=true, to_apply=%region_4.5 | all-reduce | flops 1152 | bytes 9216 | tf_op jit(solution)/shard_map/psum | solution.py:38
  (4 shorter events, 0.0 us)
Async XLA Ops:
  6.5 83.9 %reduce-scatter.4.cloned.1.call-start = ((), (), s32[]{:S(2)}) async-start(), calls=%async_computation.3 | async-start | bytes 10616832 | tf_op jit(solution)/shard_map/reduce_scatter | solution.py:23
  30.1 60.4 %copy-start.2 = (s32[256]{0:T(256)S(1)}, s32[256]{0:T(256)}, u32[]{:S(2)}) copy-start(s32[256]{0:T(256)} %param.4) | copy-start | bytes 3076
  30.1 142.1 %reduce-scatter.6.cloned.1.call-start = ((), (), s32[]{:S(2)}) async-start(), calls=%async_computation.4 | async-start | bytes 10616832 | tf_op jit(solution)/shard_map/reduce_scatter | solution.py:23
  114.9 1.3 copy-start
  114.9 139.5 %reduce-scatter.8.cloned.1.call-start = ((), (), s32[]{:S(2)}) async-start(), calls=%async_computation.5 | async-start | bytes 10616832 | tf_op jit(solution)/shard_map/reduce_scatter | solution.py:23
  197.1 0.7 copy-start.3
  197.1 57.3 %copy-start.1 = (f32[1152,256]{0,1:T(8,128)S(1)}, f32[1152,256]{0,1:T(8,128)}, u32[]{:S(2)}) copy-start(f32[1152,256]{0,1:T(8,128)} %reduce-scatter.6.cloned.1.call-done) | copy-start | bytes 3538948
  197.1 115.7 %all-gather.3.cloned.1.call-start = ((), (), s32[]{:S(2)}) async-start(), calls=%async_computation.6 | async-start | bytes 10616832 | tf_op jit(solution)/shard_map/all_gather | solution.py:33
  258.1 134.5 %all-gather.5.cloned.1.call-start = ((), (), s32[]{:S(2)}) async-start(), calls=%async_computation.7 | async-start | bytes 10616832 | tf_op jit(solution)/shard_map/all_gather | solution.py:33
  338.2 54.4 %copy-start.4 = (f32[1152,256]{0,1:T(8,128)S(1)}, f32[1152,256]{0,1:T(8,128)}, u32[]{:S(2)}) copy-start(f32[1152,256]{0,1:T(8,128)} %get-tuple-element.8) | copy-start | bytes 3538948
Sparse Core Ops, SparseCore 0:
  30.2 60.1 reduce-scatter.3
  115.0 57.1 reduce-scatter.5
  197.2 57.1 reduce-scatter.7
  258.2 54.4 all-gather.2
  338.3 54.2 all-gather.4
where the time goes:
time: 463 us; the launch traced here: 457 us
  waiting for transfers between devices  281 us (61%)
  matrix products  121 us (26%)
  blocking collectives  34.5 us (7%)
  between operations  13.2 us (3%)
    reduce_scatter x3, waiting for transfers between devices, device_program(): lax.psum_scatter(partial_counts, 'graph', scatter_dimension=0, tiled=True)  172 us
    all_gather x2, waiting for transfers between devices, device_program(): gathered = lax.all_gather(weights, 'graph', axis=0, tiled=True)  109 us
    dot_general x3, matrix products, device_program(): jnp.einsum('uv,us->vs', adj_slab, sigma, preferred_element_type=jnp.float...  72.8 us
    dot_general x2, matrix products, device_program(): jnp.einsum('uv,vs->us', adj_slab, gathered, preferred_element_type=jnp.fl...  48.4 us
    psum x1, blocking collectives, device_program(): return lax.psum(jnp.sum(total, axis=1) * scale, 'src')  34.5 us
  transfers between devices with their start and end apart: 5, of which 5 were waited for; matrix products, arithmetic and copies ran while one was open for 0% of the time, Pallas kernels for 0%

commit v1 on v0

v1 whole, which is shorter than its diff:
```python
import functools

import jax
import jax.numpy as jnp
from jax import lax
from jax.experimental import pallas as pl
from jax.experimental.pallas import tpu as pltpu
from jax.sharding import PartitionSpec as P

MESH = pl.DeviceIdType.MESH
f32, bf16 = jnp.float32, jnp.bfloat16
CHUNKS = 2
RIGHT, LEFT = 0, 1


def rows_cols(lhs, rhs):
    return lax.dot_general(lhs, rhs, (((1,), (0,)), ((), ())), preferred_element_type=f32)


def rows_rows(lhs, rhs):
    return lax.dot_general(lhs, rhs, (((1,), (1,)), ((), ())), preferred_element_type=f32)


def kernel(ring, planes, scale, adj, src, lw, out,
           a_blk, a_oth, m_oth, m_mrg, onehot, x1, x2own, x2rcv, part, wg,
           near0, far0, near, far, bc, bc_send, bc_recv, plane,
           load_sem, ssem, rsem, d2d_s, d2d_r, plane_s, plane_r):
    slab = a_oth.shape[0]
    cols_all = a_oth.shape[1]
    src_count = src.shape[0]
    m = src_count // CHUNKS
    h = m // 2
    tile = 2 * slab // 3
    ring_tiles = cols_all // tile
    blk = min(32, h)

    g = lax.axis_index("graph")
    s_me = lax.axis_index("src")
    x, c = g // 2, g % 2
    to_right = {"graph": lax.rem(x + 1, ring) * 2 + c}
    to_left = {"graph": lax.rem(x + ring - 1, ring) * 2 + c}
    to_mate = {"graph": x * 2 + (1 - c)}
    slots = (2, 1, ring - 1, 0)

    loads = []
    for i, off in enumerate(slots):
        chip = lax.rem(x + off, ring)
        at = pl.ds(pl.multiple_of((chip * 2 + (1 - c)) * slab, 128), slab)
        loads.append(pltpu.make_async_copy(adj.at[:, at], a_oth.at[:, pl.ds(i * slab, slab)], load_sem.at[i]))
    for i, off in enumerate(slots):
        chip = lax.rem(x + off, ring)
        at = pl.ds(pl.multiple_of((chip * 2 + c) * slab, 128), slab)
        loads.append(pltpu.make_async_copy(adj.at[:, at], a_blk.at[pl.ds(0, slab), pl.ds(i * slab, slab)], load_sem.at[4 + i]))
    for load in loads:
        load.start()

    barrier = pltpu.get_barrier_semaphore()
    for dev in (to_right, to_left, to_mate):
        pl.semaphore_signal(barrier, inc=1, device_id=dev, device_id_type=MESH)
    for o in range(1, planes):
        pl.semaphore_signal(barrier, inc=1, device_id={"src": lax.rem(s_me + o, planes)}, device_id_type=MESH)

    base = g * slab
    chip_base = x * 2 * slab
    ids = src[...]
    here = (ids >= base) & (ids < base + slab)
    lane = lax.broadcasted_iota(jnp.int32, (blk, slab), 1) + base

    def one_hot_rows(i, carry):
        r = pl.ds(pl.multiple_of(i * blk, blk), blk)
        onehot[r, :] = jnp.where(src[r, :] == lane, 1.0, 0.0).astype(bf16)
        return carry

    lax.fori_loop(0, src_count // blk, one_hot_rows, 0)
    bc[...] = jnp.zeros_like(bc)

    def mate_copy(i, source, target):
        return pltpu.make_async_remote_copy(src_ref=source, dst_ref=target, send_sem=d2d_s.at[i], recv_sem=d2d_r.at[i],
                                            device_id=to_mate, device_id_type=MESH)

    a_copies = [mate_copy(i, a_oth.at[:, pl.ds(i * slab, slab)], a_blk.at[pl.ds(slab, slab), pl.ds(i * slab, slab)])
                for i in range(4)]
    half_cols = [pl.ds(0, 2 * slab), pl.ds(2 * slab, 2 * slab)]
    m_copies = [mate_copy(4 + i, m_oth.at[:, half_cols[i]], m_mrg.at[:, half_cols[i]]) for i in range(2)]

    loads[0].wait()
    pl.semaphore_wait(barrier, 3 + planes - 1)
    a_copies[0].start()
    loads[1].wait()

    def select_other(t, carry):
        at = pl.ds(pl.multiple_of(t * tile, 128), tile)
        m_oth[:, at] = rows_cols(onehot[...], a_oth[:, at]).astype(bf16)
        return carry

    lax.fori_loop(0, 3, select_other, 0)
    m_copies[0].start()
    loads[2].wait()
    loads[3].wait()
    lax.fori_loop(3, 6, select_other, 0)
    m_copies[1].start()
    for i in range(1, 4):
        a_copies[i].start()

    def select_own(t, carry):
        at = pl.ds(pl.multiple_of(t * tile, 128), tile)
        mine = rows_cols(onehot[...], a_blk[pl.ds(0, slab), at])
        m_mrg[:, at] = jnp.where(here, mine, m_mrg[:, at].astype(f32)).astype(bf16)
        return carry

    for i in range(4, 8):
        loads[i].wait()
    m_copies[0].wait_recv()
    lax.fori_loop(0, 3, select_own, 0)
    m_copies[1].wait_recv()
    lax.fori_loop(3, 6, select_own, 0)

    lo, hi = pl.ds(0, h), pl.ds(h, h)
    slot = [pl.ds(i * slab, slab) for i in range(4)]
    own_half, mate_half = pl.ds(0, slab), pl.ds(slab, slab)

    def ring_copy(stage, k, way, msg, source, target):
        i = ((stage * CHUNKS + k) * 2 + way) * 3 + msg
        return pltpu.make_async_remote_copy(src_ref=source, dst_ref=target, send_sem=ssem.at[i], recv_sem=rsem.at[i],
                                            device_id=to_right if way == RIGHT else to_left, device_id_type=MESH)

    def reduce_copies(stage, k):
        if stage == 0:
            send, nr, fr = m_mrg.at[pl.ds(k * m, m), :], near0.at[k], far0.at[k]
        else:
            send, nr, fr = part.at[k], near.at[stage - 1, k], far.at[stage - 1, k]
        return {
            (RIGHT, 0): ring_copy(stage, k, RIGHT, 0, send.at[lo, slot[0]], fr.at[RIGHT]),
            (LEFT, 0): ring_copy(stage, k, LEFT, 0, send.at[hi, slot[0]], fr.at[LEFT]),
            (RIGHT, 1): ring_copy(stage, k, RIGHT, 1, send.at[hi, slot[1]], nr.at[RIGHT, hi, :]),
            (LEFT, 1): ring_copy(stage, k, LEFT, 1, send.at[lo, slot[2]], nr.at[LEFT, lo, :]),
            (RIGHT, 2): ring_copy(stage, k, RIGHT, 2, send.at[lo, slot[1]], nr.at[RIGHT, lo, :]),
            (LEFT, 2): ring_copy(stage, k, LEFT, 2, send.at[hi, slot[2]], nr.at[LEFT, hi, :]),
        }

    def gather_copies(stage, k):
        buf = wg.at[k] if stage == 3 else part.at[k]
        return {
            (RIGHT, 0): ring_copy(stage, k, RIGHT, 0, buf.at[lo, slot[3]], buf.at[lo, slot[2]]),
            (LEFT, 0): ring_copy(stage, k, LEFT, 0, buf.at[hi, slot[3]], buf.at[hi, slot[1]]),
            (RIGHT, 1): ring_copy(stage, k, RIGHT, 1, buf.at[hi, slot[3]], buf.at[hi, slot[2]]),
            (LEFT, 1): ring_copy(stage, k, LEFT, 1, buf.at[lo, slot[3]], buf.at[lo, slot[1]]),
            (RIGHT, 2): ring_copy(stage, k, RIGHT, 2, buf.at[lo, slot[2]], buf.at[lo, slot[0]]),
            (LEFT, 2): ring_copy(stage, k, LEFT, 2, buf.at[hi, slot[1]], buf.at[hi, slot[0]]),
        }

    copies = {}
    for k in range(CHUNKS):
        for stage in range(5):
            copies[stage, k] = reduce_copies(stage, k) if stage < 3 else gather_copies(stage, k)
    x1_copies = [mate_copy(6 + k, x1.at[k, :, own_half], x1.at[k, :, mate_half]) for k in range(CHUNKS)]
    x2_copies = [mate_copy(6 + CHUNKS + k, x2own.at[k], x2rcv.at[k]) for k in range(CHUNKS)]
    z_copies = [mate_copy(6 + 2 * CHUNKS + k, near.at[1, k, 1], near.at[0, k, 1]) for k in range(CHUNKS)]
    bc_copy = mate_copy(6 + 3 * CHUNKS, bc_send, bc_recv)

    def by_rows(count, fn):
        def step(i, carry):
            fn(i)
            return carry
        lax.fori_loop(0, count // blk, step, 0)

    def rows_at(i, first=0):
        return pl.ds(pl.multiple_of(first + i * blk, blk), blk)

    def start(stage, k):
        cp = copies[stage, k]
        if stage in (1, 2):
            for c_ in copies[stage - 1, k].values():
                c_.wait_send()

            def push(t, carry):
                at = pl.ds(pl.multiple_of(t * tile, 128), tile)
                if stage == 1:
                    part[k, :, at] = rows_cols(x1[k], a_blk[:, at])
                else:
                    both = rows_cols(a_oth[pl.ds(0, 2 * m), pl.ds(0, 2 * slab)], a_blk[:, at])
                    part[k, :, at] = both[:m] + both[m:]
                return carry

            lax.fori_loop(0, 3, push, 0)
            cp[RIGHT, 0].start()
            cp[LEFT, 0].start()
            cp[RIGHT, 1].start()
            lax.fori_loop(3, 6, push, 0)
            cp[LEFT, 1].start()
        else:
            for msg in (0, 1):
                cp[RIGHT, msg].start()
                cp[LEFT, msg].start()

    def middle(stage, k):
        cp = copies[stage, k]
        for way in (RIGHT, LEFT):
            cp[way, 0].wait_recv()
            first = 0 if way == RIGHT else h
            dest = slot[1] if way == RIGHT else slot[2]
            if stage == 0:
                def select(i):
                    r = pl.ds(pl.multiple_of(k * m + first + i * blk, blk), blk)
                    here_chip = (src[r, :] >= chip_base) & (src[r, :] < chip_base + 2 * slab)
                    m_mrg[r, dest] = jnp.where(here_chip, m_mrg[r, dest].astype(f32),
                                               far0[k, way, rows_at(i), :].astype(f32)).astype(bf16)
                by_rows(h, select)
            elif stage < 3:
                def add(i):
                    r = rows_at(i, first)
                    part[k, r, dest] = part[k, r, dest] + far[stage - 1, k, way, rows_at(i), :]
                by_rows(h, add)
            cp[way, 2].start()

    def pull(k, buf, use):
        def split(i):
            r = rows_at(i)
            full = buf[k, r, :]
            top = full.astype(bf16)
            rest = full - top.astype(f32)
            mid = rest.astype(bf16)
            a_oth[r, :] = top
            a_oth[rows_at(i, m), :] = mid
            a_oth[rows_at(i, 2 * m), :] = (rest - mid.astype(f32)).astype(bf16)
        by_rows(m, split)
        for t in (2, 1, 0):
            three = rows_rows(a_oth[pl.ds(0, 3 * m), :], a_blk[pl.ds(t * tile, tile), :])
            use(t, three[:m] + three[m:2 * m] + three[2 * m:])

    def finish(stage, k):
        cp = copies[stage, k]
        for way in (RIGHT, LEFT):
            cp[way, 1].wait_recv()
            cp[way, 2].wait_recv()
        if stage == 0:
            def first_level(i):
                r = rows_at(i)
                rk = rows_at(i, k * m)
                x1[k, r, own_half] = (m_mrg[rk, slot[3]].astype(f32) + near0[k, RIGHT, r, :].astype(f32)
                                      + near0[k, LEFT, r, :].astype(f32)).astype(bf16)
            by_rows(m, first_level)
            x1_copies[k].start()
            for i in range(4):
                if k == 0:
                    a_copies[i].wait_recv()
            x1_copies[k].wait_recv()
        elif stage == 1:
            def second_level(i):
                r = rows_at(i)
                rk = rows_at(i, k * m)
                total = part[k, r, slot[3]] + near[0, k, RIGHT, r, :] + near[0, k, LEFT, r, :]
                seen = jnp.maximum(onehot[rk, :].astype(f32), x1[k, r, own_half].astype(f32))
                x2own[k, r, :] = total * (1.0 - seen)
            by_rows(m, second_level)
            x2_copies[k].start()
            if k == 0:
                for copy in a_copies:
                    copy.wait_send()

            def split(i, source, half):
                r = rows_at(i)
                full = source[k, r, :]
                top = full.astype(bf16)
                a_oth[r, half] = top
                a_oth[rows_at(i, m), half] = (full - top.astype(f32)).astype(bf16)
            by_rows(m, lambda i: split(i, x2own, own_half))
            x2_copies[k].wait_recv()
            by_rows(m, lambda i: split(i, x2rcv, mate_half))
        elif stage == 2:
            def third_level(i):
                r = rows_at(i)
                rk = rows_at(i, k * m)
                total = part[k, r, slot[3]] + near[1, k, RIGHT, r, :] + near[1, k, LEFT, r, :]
                seen = jnp.maximum(onehot[rk, :].astype(f32), x1[k, r, own_half].astype(f32))
                seen = jnp.maximum(seen, jnp.where(x2own[k, r, :] > 0, 1.0, 0.0))
                paths = total * (1.0 - seen)
                reached = paths > 0
                wg[k, r, slot[3]] = jnp.where(reached, lw[1] / jnp.where(reached, paths, 1.0), 0.0)
            by_rows(m, third_level)
            for c_ in cp.values():
                c_.wait_send()
        elif stage == 3:
            mine, theirs = near.at[1, k, 0], near.at[1, k, 1]

            def keep(t, z):
                first = t * tile
                if first >= slab:
                    theirs[:, pl.ds(first - slab, tile)] = z
                elif first + tile > slab:
                    cut = slab - first
                    mine[:, pl.ds(first, cut)] = z[:, :cut]
                    theirs[:, pl.ds(0, tile - cut)] = z[:, cut:]
                    z_copies[k].start()
                else:
                    mine[:, pl.ds(first, tile)] = z
            pull(k, wg, keep)
            z_copies[k].wait_recv()

            def second_weights(i):
                r = rows_at(i)
                paths = x2own[k, r, :]
                delta = paths * (mine[r, :] + near[0, k, 1, r, :])
                reached = paths > 0
                part[k, r, slot[3]] = jnp.where(reached, (lw[0] + delta) / jnp.where(reached, paths, 1.0), 0.0)
                bc[:, own_half] = bc[:, own_half] + jnp.sum(delta, axis=0, keepdims=True)
            by_rows(m, second_weights)
        else:
            def close(t, z):
                at = pl.ds(t * tile, tile)
                bc[:, at] = bc[:, at] + jnp.sum(x1[k, :, at].astype(f32) * z, axis=0, keepdims=True)
            pull(k, part, close)

    for k in range(CHUNKS):
        start(0, k)
    for k in range(CHUNKS):
        middle(0, k)
    for stage in range(1, 5):
        for k in range(CHUNKS):
            finish(stage - 1, k)
            start(stage, k)
            middle(stage, k)
    for k in range(CHUNKS):
        finish(4, k)

    bc_send[...] = bc[:, mate_half]
    bc_copy.start()
    bc_copy.wait_recv()
    plane[pl.ds(s_me, 1)] = ((bc[:, own_half] + bc_recv[...]) * scale)[None]
    plane_copies = []
    for o in range(1, planes):
        copy = pltpu.make_async_remote_copy(src_ref=plane.at[s_me], dst_ref=plane.at[s_me], send_sem=plane_s.at[o],
                                            recv_sem=plane_r.at[o],
                                            device_id={"src": lax.rem(s_me + o, planes)}, device_id_type=MESH)
        copy.start()
        plane_copies.append(copy)
    for o in range(1, planes):
        arrived = plane.at[lax.rem(s_me + planes - o, planes)]
        pltpu.make_async_remote_copy(src_ref=arrived, dst_ref=arrived, send_sem=plane_s.at[o], recv_sem=plane_r.at[o],
                                     device_id={"src": lax.rem(s_me + o, planes)}, device_id_type=MESH).wait_recv()
    out[...] = jnp.sum(plane[...], axis=0)

    for copy in plane_copies + m_copies + x1_copies + x2_copies + z_copies + [bc_copy]:
        copy.wait_send()
    for k in range(CHUNKS):
        for stage in (3, 4):
            for c_ in copies[stage, k].values():
                c_.wait_send()


def solution(mesh):
    planes = mesh.shape["src"]
    ring = mesh.shape["graph"] // 2

    def device_program(adj_slab, src_local, level_weight):
        slab, vertex_count = adj_slab.shape
        src_count = src_local.shape[0]
        m = src_count // CHUNKS
        scale = vertex_count / (src_count * planes * (level_weight.shape[0] + 1) ** 3)
        wide = 4 * slab
        vmem = pltpu.VMEM
        sem = pltpu.SemaphoreType.DMA
        mates = 7 + 3 * CHUNKS
        rings = 5 * CHUNKS * 6
        flops = 2 * 9 * src_count * slab * vertex_count
        bc = pl.pallas_call(
            functools.partial(kernel, ring, planes, scale),
            out_shape=jax.ShapeDtypeStruct((1, slab), f32),
            in_specs=[pl.BlockSpec(memory_space=pl.ANY), pl.BlockSpec(memory_space=vmem), pl.BlockSpec(memory_space=pltpu.SMEM)],
            out_specs=pl.BlockSpec(memory_space=vmem),
            scratch_shapes=[
                vmem((2 * slab, wide), bf16), vmem((slab, wide), bf16),
                vmem((src_count, wide), bf16), vmem((src_count, wide), bf16), vmem((src_count, slab), bf16),
                vmem((CHUNKS, m, 2 * slab), bf16), vmem((CHUNKS, m, slab), f32), vmem((CHUNKS, m, slab), f32),
                vmem((CHUNKS, m, wide), f32), vmem((CHUNKS, m, wide), f32),
                vmem((CHUNKS, 2, m, slab), bf16), vmem((CHUNKS, 2, m // 2, slab), bf16),
                vmem((2, CHUNKS, 2, m, slab), f32), vmem((2, CHUNKS, 2, m // 2, slab), f32),
                vmem((1, 2 * slab), f32), vmem((1, slab), f32), vmem((1, slab), f32), vmem((planes, 1, slab), f32),
                sem((8,)), sem((rings,)), sem((rings,)), sem((mates,)), sem((mates,)), sem((planes,)), sem((planes,)),
            ],
            compiler_params=pltpu.CompilerParams(collective_id=0, has_side_effects=True, vmem_limit_bytes=67043328),
            cost_estimate=pl.CostEstimate(flops=flops, bytes_accessed=2 * slab * vertex_count, transcendentals=0),
        )(adj_slab, src_local.reshape(src_count, 1), level_weight)
        return bc.reshape(slab)

    return jax.shard_map(device_program, mesh=mesh,
                         in_specs=(P(("batch", "graph"), None), P(("batch", "src")), P(None)),
                         out_specs=P(("batch", "graph")), check_vma=False)
```

time: 463 us -> 216 us (0.47); the launches traced: 457 us -> 216 us
  waiting for transfers between devices: 281 us -> 0 us
  Pallas kernels: 0 us -> 213 us
  matrix products: 121 us -> 0 us
  blocking collectives: 34.5 us -> 0 us
  between operations: 13.2 us -> 0.01 us
    pallas_call x0 -> x1, Pallas kernels: none -> 213 us  [device_program(): pl.pallas_call(functools.partial(kernel, ring, planes, scale), out_shape=...]
    reduce_scatter x3 -> x0, waiting for transfers between devices: 172 us -> none  [device_program(): lax.psum_scatter(partial_counts, 'graph', scatter_dimension=0, tiled=True)]
    dot_general x5 -> x0, matrix products: 121 us -> none  [the longest x3 72.8 us: device_program(): jnp.einsum('uv,us->vs', adj_slab, sigma, preferred_element_type=jnp.float...]
    all_gather x2 -> x0, waiting for transfers between devices: 109 us -> none  [device_program(): gathered = lax.all_gather(weights, 'graph', axis=0, tiled=True)]
    psum x1 -> x0, blocking collectives: 34.5 us -> none  [device_program(): return lax.psum(jnp.sum(total, axis=1) * scale, 'src')]
  transfers between devices with their start and end apart: 5 -> 0, of which waited for: 5 -> 0; matrix products, arithmetic and copies ran while one was open for 0% -> 0% of each run, Pallas kernels for 0% -> 0%
where the time goes in v1:
time: 216 us
  Pallas kernels  213 us (99%)
    pallas_call x1, Pallas kernels, device_program(): pl.pallas_call(functools.partial(kernel, ring, planes, scale), out_shape=...  213 us

profile of v1, /device:TPU:1, one launch (start us, length us, event | category | flops | bytes accessed | tf_op | source)
XLA Modules:
  0.0 215.7 jit_solution(4747005908271365133)
XLA Ops:
  0.0 1.5 copy.4.src
  1.5 213.0 %shard_map.37 = f32[1,1152]{1,0:T(1,128)} custom-call(bf16[1152,9216]{1,0:T(8,128)(2,1)} %adj.1, s32[256,1]{1,0:T(8,128)} %copy.4.src, f32[2]{0:T(128)} %lw.1), custom_call_target="tpu_custom_call" | custom-call | flops 48922361856 | bytes 21233664 | tf_op jit(solution)/shard_map/pallas_call | solution.py:366
  214.4 1.3 reduce

commit v2 on v1

v2 whole, which is shorter than its diff:
```python
import functools

import jax
import jax.numpy as jnp
from jax import lax
from jax.experimental import pallas as pl
from jax.experimental.pallas import tpu as pltpu
from jax.sharding import PartitionSpec as P

MESH = pl.DeviceIdType.MESH
f32, bf16 = jnp.float32, jnp.bfloat16
CHUNKS = 2
TO_P, TO_Q = 0, 1


def rows_cols(lhs, rhs):
    return lax.dot_general(lhs, rhs, (((1,), (0,)), ((), ())), preferred_element_type=f32)


def rows_rows(lhs, rhs):
    return lax.dot_general(lhs, rhs, (((1,), (1,)), ((), ())), preferred_element_type=f32)


def kernel(ring, planes, scale, adj, src, lw, out,
           a_blk, a_oth, pick, ids, onehot, x1, x2own, x2rcv, part, wg,
           near0, far0, near, far, bc, bc_send, bc_recv, plane,
           load_sem, ssem, rsem, d2d_s, d2d_r, plane_s, plane_r):
    slab = a_oth.shape[0]
    cols_all = a_oth.shape[1]
    src_count = ids.shape[0]
    m = src_count // CHUNKS
    h = m // 2
    tile = 2 * slab // 3
    blk = min(32, h)

    g = lax.axis_index("graph")
    s_me = lax.axis_index("src")
    x, c = g // 2, g % 2
    odd = lax.rem(x, 2)
    chip_p = x + 1 - 2 * odd
    chip_q = lax.rem(x + ring - 1 + 2 * odd, ring)
    chip_far = lax.rem(x + 2, ring)
    to_p = {"graph": chip_p * 2 + c}
    to_q = {"graph": chip_q * 2 + c}
    to_mate = {"graph": x * 2 + (1 - c)}
    chips = (chip_far, chip_p, chip_q, x)
    slot = [pl.ds(i * slab, slab) for i in range(4)]
    FAR, NEAR_P, NEAR_Q, OWN = slot

    loads = {}
    for i, chip in enumerate(chips):
        for own in (0, 1):
            at = pl.ds(pl.multiple_of((chip * 2 + (c if own else 1 - c)) * slab, 128), slab)
            target = a_blk.at[pl.ds(0, slab), slot[i]] if own else a_oth.at[:, slot[i]]
            loads[own, i] = pltpu.make_async_copy(adj.at[:, at], target, load_sem.at[4 * own + i])
    for pair in ((0, 1), (2, 3)):
        for own in (0, 1):
            for i in pair:
                loads[own, i].start()

    barrier = pltpu.get_barrier_semaphore()
    for dev in (to_p, to_q, to_mate):
        pl.semaphore_signal(barrier, inc=1, device_id=dev, device_id_type=MESH)
    for o in range(1, planes):
        pl.semaphore_signal(barrier, inc=1, device_id={"src": lax.rem(s_me + o, planes)}, device_id_type=MESH)

    row = lax.broadcasted_iota(jnp.int32, (src_count, src_count), 0)
    col = lax.broadcasted_iota(jnp.int32, (src_count, src_count), 1)
    ids[...] = jnp.sum(jnp.where(row == col, src[...].astype(f32), 0.0), axis=1, keepdims=True)
    base = g * slab
    base_f = base.astype(f32)
    chip_f = (x * 2 * slab).astype(f32)
    lane = (lax.broadcasted_iota(jnp.int32, (blk, slab), 1) + base).astype(f32)

    def one_hot_rows(i, carry):
        r = pl.ds(pl.multiple_of(i * blk, blk), blk)
        onehot[r, :] = jnp.where(ids[r, :] == lane, 1.0, 0.0).astype(bf16)
        return carry

    lax.fori_loop(0, src_count // blk, one_hot_rows, 0)
    bc[...] = jnp.zeros_like(bc)

    def mate_copy(i, source, target):
        return pltpu.make_async_remote_copy(src_ref=source, dst_ref=target, send_sem=d2d_s.at[i], recv_sem=d2d_r.at[i],
                                            device_id=to_mate, device_id_type=MESH)

    def ring_copy(stage, k, way, msg, source, target):
        i = ((stage * CHUNKS + k) * 2 + way) * 3 + msg
        return pltpu.make_async_remote_copy(src_ref=source, dst_ref=target, send_sem=ssem.at[i], recv_sem=rsem.at[i],
                                            device_id=to_p if way == TO_P else to_q, device_id_type=MESH)

    lo, hi = pl.ds(0, h), pl.ds(h, h)
    side = [pl.ds(0, slab), pl.ds(slab, slab)]
    own_half, mate_half = side
    merged = [pick.at[pl.ds(src_count + k * m, m), :] for k in range(CHUNKS)]
    two = [pl.ds(0, 2 * slab), pl.ds(2 * slab, 2 * slab)]

    def reduce_copies(stage, k):
        if stage == 0:
            send, nr, fr = merged[k], near0.at[k], far0.at[k]
        else:
            send, nr, fr = part.at[k], near.at[stage - 1, k], far.at[stage - 1, k]
        return {
            (TO_P, 0): ring_copy(stage, k, TO_P, 0, send.at[lo, FAR], fr.at[TO_P]),
            (TO_Q, 0): ring_copy(stage, k, TO_Q, 0, send.at[hi, FAR], fr.at[TO_Q]),
            (TO_P, 1): ring_copy(stage, k, TO_P, 1, send.at[lo, NEAR_P], nr.at[lo, side[TO_P]]),
            (TO_Q, 1): ring_copy(stage, k, TO_Q, 1, send.at[hi, NEAR_Q], nr.at[hi, side[TO_Q]]),
            (TO_P, 2): ring_copy(stage, k, TO_P, 2, send.at[hi, NEAR_P], nr.at[hi, side[TO_P]]),
            (TO_Q, 2): ring_copy(stage, k, TO_Q, 2, send.at[lo, NEAR_Q], nr.at[lo, side[TO_Q]]),
        }

    def gather_copies(stage, k):
        buf = wg.at[k] if stage == 3 else part.at[k]
        return {
            (TO_P, 0): ring_copy(stage, k, TO_P, 0, buf.at[lo, OWN], buf.at[lo, NEAR_P]),
            (TO_Q, 0): ring_copy(stage, k, TO_Q, 0, buf.at[hi, OWN], buf.at[hi, NEAR_Q]),
            (TO_P, 1): ring_copy(stage, k, TO_P, 1, buf.at[hi, OWN], buf.at[hi, NEAR_P]),
            (TO_Q, 1): ring_copy(stage, k, TO_Q, 1, buf.at[lo, OWN], buf.at[lo, NEAR_Q]),
            (TO_P, 2): ring_copy(stage, k, TO_P, 2, buf.at[hi, NEAR_Q], buf.at[hi, FAR]),
            (TO_Q, 2): ring_copy(stage, k, TO_Q, 2, buf.at[lo, NEAR_P], buf.at[lo, FAR]),
        }

    copies = {}
    for k in range(CHUNKS):
        for stage in range(5):
            copies[stage, k] = reduce_copies(stage, k) if stage < 3 else gather_copies(stage, k)
    a_copies = [mate_copy(i, a_oth.at[:, slot[i]], a_blk.at[pl.ds(slab, slab), slot[i]]) for i in range(4)]
    m_copies = {(k, i): mate_copy(4 + 2 * k + i, pick.at[pl.ds(k * m, m), two[i]], merged[k].at[:, two[i]])
                for k in range(CHUNKS) for i in range(2)}
    first = 4 + 2 * CHUNKS
    x1_copies = [mate_copy(first + k, x1.at[k, :, own_half], x1.at[k, :, mate_half]) for k in range(CHUNKS)]
    x2_copies = [mate_copy(first + CHUNKS + k, x2own.at[k], x2rcv.at[k]) for k in range(CHUNKS)]
    z_copies = [mate_copy(first + 2 * CHUNKS + k, near.at[1, k, :, mate_half], near.at[0, k, :, mate_half]) for k in range(CHUNKS)]
    bc_copy = mate_copy(first + 3 * CHUNKS, bc_send, bc_recv)

    def by_rows(count, fn):
        def step(i, carry):
            fn(i)
            return carry
        lax.fori_loop(0, count // blk, step, 0)

    def rows_at(i, start=0):
        return pl.ds(pl.multiple_of(start + i * blk, blk), blk)

    def by_tiles(begin, end, fn):
        def step(t, carry):
            fn(pl.ds(pl.multiple_of(t * tile, 128), tile))
            return carry
        lax.fori_loop(begin, end, step, 0)

    def select_other(k, i):
        def one(at):
            pick[pl.ds(k * m, m), at] = rows_cols(onehot[pl.ds(k * m, m), :], a_oth[:, at]).astype(bf16)
        by_tiles(3 * i, 3 * i + 3, one)
        m_copies[k, i].start()

    def select_own(k, i):
        rk = pl.ds(k * m, m)
        here = (ids[rk, :] >= base_f) & (ids[rk, :] < base_f + slab)

        def one(at):
            mine = rows_cols(onehot[rk, :], a_blk[pl.ds(0, slab), at])
            merged[k][:, at] = jnp.where(here, mine, merged[k][:, at].astype(f32)).astype(bf16)
        m_copies[k, i].wait_recv()
        by_tiles(3 * i, 3 * i + 3, one)

    def send_first(stage, k):
        cp = copies[stage, k]
        cp[TO_P, 0].start()
        cp[TO_Q, 0].start()
        cp[TO_P, 1].start()

    def start(stage, k):
        cp = copies[stage, k]
        if stage in (1, 2):
            for c_ in copies[stage - 1, k].values():
                c_.wait_send()

            def push(at):
                if stage == 1:
                    part[k, :, at] = rows_cols(x1[k], a_blk[:, at])
                else:
                    both = rows_cols(pick[pl.ds(0, 2 * m), two[0]], a_blk[:, at])
                    part[k, :, at] = both[:m] + both[m:]

            by_tiles(0, 3, push)
            send_first(stage, k)
            by_tiles(3, 6, push)
            cp[TO_Q, 1].start()
        else:
            for msg in (0, 1):
                cp[TO_P, msg].start()
                cp[TO_Q, msg].start()

    def middle(stage, k):
        cp = copies[stage, k]
        for way in (TO_P, TO_Q):
            cp[way, 0].wait_recv()
            begin = 0 if way == TO_P else h
            dest = NEAR_Q if way == TO_P else NEAR_P
            if stage == 0:
                def select(i):
                    r = rows_at(i, begin)
                    rk = rows_at(i, k * m + begin)
                    here = (ids[rk, :] >= chip_f) & (ids[rk, :] < chip_f + 2 * slab)
                    merged[k][r, dest] = jnp.where(here, merged[k][r, dest].astype(f32),
                                                   far0[k, way, rows_at(i), :].astype(f32)).astype(bf16)
                by_rows(h, select)
            elif stage < 3:
                def add(i):
                    r = rows_at(i, begin)
                    part[k, r, dest] = part[k, r, dest] + far[stage - 1, k, way, rows_at(i), :]
                by_rows(h, add)
            cp[1 - way, 2].start()

    def pull(buf, k, at, use):
        def split(i):
            r = rows_at(i)
            full = buf[k, r, at]
            top = full.astype(bf16)
            rest = full - top.astype(f32)
            mid = rest.astype(bf16)
            pick[r, at] = top
            pick[rows_at(i, m), at] = mid
            pick[rows_at(i, 2 * m), at] = (rest - mid.astype(f32)).astype(bf16)
        by_rows(m, split)
        for t in (2, 1, 0):
            three = rows_rows(pick[pl.ds(0, 3 * m), at], a_blk[pl.ds(t * tile, tile), at])
            use(t, three[:m] + three[m:2 * m] + three[2 * m:])

    def close(k, t, z):
        at = pl.ds(t * tile, tile)
        bc[:, at] = bc[:, at] + jnp.sum(x1[k, :, at].astype(f32) * z, axis=0, keepdims=True)

    def nears(stage, k):
        cp = copies[stage, k]
        cp[TO_P, 1].wait_recv()
        cp[TO_Q, 1].wait_recv()

        def keep(t, z):
            if stage == 3:
                near[1, k, :, pl.ds(t * tile, tile)] = z
            else:
                close(k, t, z)
        pull(wg if stage == 3 else part, k, pl.ds(slab, 3 * slab), keep)

    def finish(stage, k):
        cp = copies[stage, k]
        for way in (TO_P, TO_Q):
            if stage < 3:
                cp[way, 1].wait_recv()
            cp[way, 2].wait_recv()
        if stage == 0:
            def first_level(i):
                r = rows_at(i)
                x1[k, r, own_half] = (merged[k][r, OWN].astype(f32) + near0[k, r, side[0]].astype(f32)
                                      + near0[k, r, side[1]].astype(f32)).astype(bf16)
            by_rows(m, first_level)
            x1_copies[k].start()
            if k == 0:
                for copy in a_copies:
                    copy.wait_recv()
                for copy in m_copies.values():
                    copy.wait_send()
            x1_copies[k].wait_recv()
        elif stage == 1:
            def second_level(i):
                r = rows_at(i)
                rk = rows_at(i, k * m)
                total = part[k, r, OWN] + near[0, k, r, side[0]] + near[0, k, r, side[1]]
                seen = jnp.maximum(onehot[rk, :].astype(f32), x1[k, r, own_half].astype(f32))
                x2own[k, r, :] = total * (1.0 - seen)
            by_rows(m, second_level)
            x2_copies[k].start()

            def split(i, source, half):
                r = rows_at(i)
                full = source[k, r, :]
                top = full.astype(bf16)
                pick[r, half] = top
                pick[rows_at(i, m), half] = (full - top.astype(f32)).astype(bf16)
            by_rows(m, lambda i: split(i, x2own, own_half))
            x2_copies[k].wait_recv()
            by_rows(m, lambda i: split(i, x2rcv, mate_half))
        elif stage == 2:
            def third_level(i):
                r = rows_at(i)
                rk = rows_at(i, k * m)
                total = part[k, r, OWN] + near[1, k, r, side[0]] + near[1, k, r, side[1]]
                seen = jnp.maximum(onehot[rk, :].astype(f32), x1[k, r, own_half].astype(f32))
                seen = jnp.maximum(seen, jnp.where(x2own[k, r, :] > 0, 1.0, 0.0))
                paths = total * (1.0 - seen)
                reached = paths > 0
                wg[k, r, OWN] = jnp.where(reached, lw[1] / jnp.where(reached, paths, 1.0), 0.0)
            by_rows(m, third_level)
            for c_ in cp.values():
                c_.wait_send()
        elif stage == 3:
            def keep(t, z):
                at = pl.ds(t * tile, tile)
                near[1, k, :, at] = near[1, k, :, at] + z
                if t == 1:
                    z_copies[k].start()
            pull(wg, k, FAR, keep)
            z_copies[k].wait_recv()

            def second_weights(i):
                r = rows_at(i)
                paths = x2own[k, r, :]
                delta = paths * (near[1, k, r, own_half] + near[0, k, r, mate_half])
                reached = paths > 0
                part[k, r, OWN] = jnp.where(reached, (lw[0] + delta) / jnp.where(reached, paths, 1.0), 0.0)
                bc[:, own_half] = bc[:, own_half] + jnp.sum(delta, axis=0, keepdims=True)
            by_rows(m, second_weights)
        else:
            pull(part, k, FAR, functools.partial(close, k))

    loads[0, 0].wait()
    loads[0, 1].wait()
    pl.semaphore_wait(barrier, 3 + planes - 1)
    for k in range(CHUNKS):
        select_other(k, 0)
    loads[1, 0].wait()
    loads[1, 1].wait()
    for k in range(CHUNKS):
        select_own(k, 0)
        send_first(0, k)
    loads[0, 2].wait()
    loads[0, 3].wait()
    for k in range(CHUNKS):
        select_other(k, 1)
    for copy in a_copies:
        copy.start()
    loads[1, 2].wait()
    loads[1, 3].wait()
    for k in range(CHUNKS):
        select_own(k, 1)
        copies[0, k][TO_Q, 1].start()
    for k in range(CHUNKS):
        middle(0, k)
    for stage in range(1, 5):
        finish(stage - 1, 0)
        start(stage, 0)
        if stage == 4:
            nears(3, 1)
        middle(stage, 0)
        finish(stage - 1, 1)
        start(stage, 1)
        if stage >= 3:
            nears(stage, 0)
        middle(stage, 1)
    finish(4, 0)
    nears(4, 1)
    finish(4, 1)

    bc_send[...] = bc[:, mate_half]
    bc_copy.start()
    bc_copy.wait_recv()
    plane[pl.ds(s_me, 1)] = ((bc[:, own_half] + bc_recv[...]) * scale)[None]
    plane_copies = []
    for o in range(1, planes):
        copy = pltpu.make_async_remote_copy(src_ref=plane.at[s_me], dst_ref=plane.at[s_me], send_sem=plane_s.at[o],
                                            recv_sem=plane_r.at[o],
                                            device_id={"src": lax.rem(s_me + o, planes)}, device_id_type=MESH)
        copy.start()
        plane_copies.append(copy)
    for o in range(1, planes):
        arrived = plane.at[lax.rem(s_me + planes - o, planes)]
        pltpu.make_async_remote_copy(src_ref=arrived, dst_ref=arrived, send_sem=plane_s.at[o], recv_sem=plane_r.at[o],
                                     device_id={"src": lax.rem(s_me + o, planes)}, device_id_type=MESH).wait_recv()
    out[...] = jnp.sum(plane[...], axis=0)

    for copy in plane_copies + a_copies + x1_copies + x2_copies + z_copies + [bc_copy]:
        copy.wait_send()
    for k in range(CHUNKS):
        for stage in (3, 4):
            for c_ in copies[stage, k].values():
                c_.wait_send()


def solution(mesh):
    planes = mesh.shape["src"]
    ring = mesh.shape["graph"] // 2

    def device_program(adj_slab, src_local, level_weight):
        slab, vertex_count = adj_slab.shape
        src_count = src_local.shape[0]
        m = src_count // CHUNKS
        scale = vertex_count / (src_count * planes * (level_weight.shape[0] + 1) ** 3)
        wide = 4 * slab
        vmem = pltpu.VMEM
        sem = pltpu.SemaphoreType.DMA
        mates = 5 + 5 * CHUNKS
        rings = 5 * CHUNKS * 6
        flops = 2 * 9 * src_count * slab * vertex_count
        bc = pl.pallas_call(
            functools.partial(kernel, ring, planes, scale),
            out_shape=jax.ShapeDtypeStruct((1, slab), f32),
            in_specs=[pl.BlockSpec(memory_space=pl.ANY), pl.BlockSpec(memory_space=vmem), pl.BlockSpec(memory_space=pltpu.SMEM)],
            out_specs=pl.BlockSpec(memory_space=vmem),
            scratch_shapes=[
                vmem((2 * slab, wide), bf16), vmem((slab, wide), bf16),
                vmem((2 * src_count, wide), bf16), vmem((src_count, 1), f32), vmem((src_count, slab), bf16),
                vmem((CHUNKS, m, 2 * slab), bf16), vmem((CHUNKS, m, slab), f32), vmem((CHUNKS, m, slab), f32),
                vmem((CHUNKS, m, wide), f32), vmem((CHUNKS, m, wide), f32),
                vmem((CHUNKS, m, 2 * slab), bf16), vmem((CHUNKS, 2, m // 2, slab), bf16),
                vmem((2, CHUNKS, m, 2 * slab), f32), vmem((2, CHUNKS, 2, m // 2, slab), f32),
                vmem((1, 2 * slab), f32), vmem((1, slab), f32), vmem((1, slab), f32), vmem((planes, 1, slab), f32),
                sem((8,)), sem((rings,)), sem((rings,)), sem((mates,)), sem((mates,)), sem((planes,)), sem((planes,)),
            ],
            compiler_params=pltpu.CompilerParams(collective_id=0, has_side_effects=True, vmem_limit_bytes=67043328),
            cost_estimate=pl.CostEstimate(flops=flops, bytes_accessed=2 * slab * vertex_count, transcendentals=0),
        )(adj_slab, src_local.reshape(1, src_count), level_weight)
        return bc.reshape(slab)

    return jax.shard_map(device_program, mesh=mesh,
                         in_specs=(P(("batch", "graph"), None), P(("batch", "src")), P(None)),
                         out_specs=P(("batch", "graph")), check_vma=False)
```

time: 216 us -> 205 us (0.949)
  Pallas kernels: 213 us -> 204 us
    pallas_call x1, Pallas kernels: 213 us -> 204 us  [device_program(): pl.pallas_call(functools.partial(kernel, ring, planes, scale), out_shape=...]
where the time goes in v2:
time: 205 us
  Pallas kernels  204 us (100%)
    pallas_call x1, Pallas kernels, device_program(): pl.pallas_call(functools.partial(kernel, ring, planes, scale), out_shape=...  204 us

profile of v2, /device:TPU:1, one launch (start us, length us, event | category | flops | bytes accessed | tf_op | source)
XLA Modules:
  0.0 205.2 jit_solution(15980213565525356279)
XLA Ops:
  0.0 203.9 %shard_map.37 = f32[1,1152]{1,0:T(1,128)} custom-call(bf16[1152,9216]{1,0:T(8,128)(2,1)} %adj.1, s32[1,256]{1,0:T(1,128)} %bitcast.1, f32[2]{0:T(128)} %lw.1), custom_call_target="tpu_custom_call" | custom-call | flops 48922361856 | bytes 21233664 | tf_op jit(solution)/shard_map/pallas_call | solution.py:396
  203.9 1.3 reduce

commit v3 on v2

--- a/solution.py
+++ b/solution.py
@@ -23,7 +23,7 @@
 
 def kernel(ring, planes, scale, adj, src, lw, out,
            a_blk, a_oth, pick, ids, onehot, x1, x2own, x2rcv, part, wg,
-           near0, far0, near, far, bc, bc_send, bc_recv, plane,
+           near0, far0, near, far, bc, total, plane,
            load_sem, ssem, rsem, d2d_s, d2d_r, plane_s, plane_r):
     slab = a_oth.shape[0]
     cols_all = a_oth.shape[1]
@@ -53,16 +53,16 @@
             at = pl.ds(pl.multiple_of((chip * 2 + (c if own else 1 - c)) * slab, 128), slab)
             target = a_blk.at[pl.ds(0, slab), slot[i]] if own else a_oth.at[:, slot[i]]
             loads[own, i] = pltpu.make_async_copy(adj.at[:, at], target, load_sem.at[4 * own + i])
-    for pair in ((0, 1), (2, 3)):
-        for own in (0, 1):
-            for i in pair:
-                loads[own, i].start()
+    for own, i in ((0, 0), (0, 1), (1, 0), (1, 1), (0, 2), (1, 2), (0, 3), (1, 3)):
+        loads[own, i].start()
 
     barrier = pltpu.get_barrier_semaphore()
     for dev in (to_p, to_q, to_mate):
         pl.semaphore_signal(barrier, inc=1, device_id=dev, device_id_type=MESH)
     for o in range(1, planes):
-        pl.semaphore_signal(barrier, inc=1, device_id={"src": lax.rem(s_me + o, planes)}, device_id_type=MESH)
+        there = lax.rem(s_me + o, planes)
+        pl.semaphore_signal(barrier, inc=1, device_id={"src": there}, device_id_type=MESH)
+        pl.semaphore_signal(barrier, inc=1, device_id={"src": there, "graph": x * 2 + (1 - c)}, device_id_type=MESH)
 
     row = lax.broadcasted_iota(jnp.int32, (src_count, src_count), 0)
     col = lax.broadcasted_iota(jnp.int32, (src_count, src_count), 1)
@@ -125,13 +125,12 @@
         for stage in range(5):
             copies[stage, k] = reduce_copies(stage, k) if stage < 3 else gather_copies(stage, k)
     a_copies = [mate_copy(i, a_oth.at[:, slot[i]], a_blk.at[pl.ds(slab, slab), slot[i]]) for i in range(4)]
-    m_copies = {(k, i): mate_copy(4 + 2 * k + i, pick.at[pl.ds(k * m, m), two[i]], merged[k].at[:, two[i]])
-                for k in range(CHUNKS) for i in range(2)}
-    first = 4 + 2 * CHUNKS
+    m_copies = {(k, i): mate_copy(4 + 4 * k + i, pick.at[pl.ds(k * m, m), slot[i]], merged[k].at[:, slot[i]])
+                for k in range(CHUNKS) for i in range(4)}
+    first = 4 + 4 * CHUNKS
     x1_copies = [mate_copy(first + k, x1.at[k, :, own_half], x1.at[k, :, mate_half]) for k in range(CHUNKS)]
     x2_copies = [mate_copy(first + CHUNKS + k, x2own.at[k], x2rcv.at[k]) for k in range(CHUNKS)]
     z_copies = [mate_copy(first + 2 * CHUNKS + k, near.at[1, k, :, mate_half], near.at[0, k, :, mate_half]) for k in range(CHUNKS)]
-    bc_copy = mate_copy(first + 3 * CHUNKS, bc_send, bc_recv)
 
     def by_rows(count, fn):
         def step(i, carry):
@@ -149,20 +148,14 @@
         lax.fori_loop(begin, end, step, 0)
 
     def select_other(k, i):
-        def one(at):
-            pick[pl.ds(k * m, m), at] = rows_cols(onehot[pl.ds(k * m, m), :], a_oth[:, at]).astype(bf16)
-        by_tiles(3 * i, 3 * i + 3, one)
-        m_copies[k, i].start()
+        pick[pl.ds(k * m, m), slot[i]] = rows_cols(onehot[pl.ds(k * m, m), :], a_oth[:, slot[i]]).astype(bf16)
 
     def select_own(k, i):
         rk = pl.ds(k * m, m)
         here = (ids[rk, :] >= base_f) & (ids[rk, :] < base_f + slab)
-
-        def one(at):
-            mine = rows_cols(onehot[rk, :], a_blk[pl.ds(0, slab), at])
-            merged[k][:, at] = jnp.where(here, mine, merged[k][:, at].astype(f32)).astype(bf16)
         m_copies[k, i].wait_recv()
-        by_tiles(3 * i, 3 * i + 3, one)
+        mine = rows_cols(onehot[rk, :], a_blk[pl.ds(0, slab), slot[i]])
+        merged[k][:, slot[i]] = jnp.where(here, mine, merged[k][:, slot[i]].astype(f32)).astype(bf16)
 
     def send_first(stage, k):
         cp = copies[stage, k]
@@ -213,7 +206,7 @@
                 by_rows(h, add)
             cp[1 - way, 2].start()
 
-    def pull(buf, k, at, use):
+    def pull(buf, k, at, use, meanwhile=None):
         def split(i):
             r = rows_at(i)
             full = buf[k, r, at]
@@ -224,12 +217,18 @@
             pick[rows_at(i, m), at] = mid
             pick[rows_at(i, 2 * m), at] = (rest - mid.astype(f32)).astype(bf16)
         by_rows(m, split)
-        for t in (2, 1, 0):
-            three = rows_rows(pick[pl.ds(0, 3 * m), at], a_blk[pl.ds(t * tile, tile), at])
-            use(t, three[:m] + three[m:2 * m] + three[2 * m:])
-
-    def close(k, t, z):
-        at = pl.ds(t * tile, tile)
+
+        def product(r):
+            three = rows_rows(pick[pl.ds(0, 3 * m), at], a_blk[r, at])
+            use(r, three[:m] + three[m:2 * m] + three[2 * m:])
+        if meanwhile is None:
+            by_tiles(0, 3, product)
+        else:
+            by_tiles(1, 3, product)
+            meanwhile()
+            by_tiles(0, 1, product)
+
+    def close(k, at, z):
         bc[:, at] = bc[:, at] + jnp.sum(x1[k, :, at].astype(f32) * z, axis=0, keepdims=True)
 
     def nears(stage, k):
@@ -237,11 +236,11 @@
         cp[TO_P, 1].wait_recv()
         cp[TO_Q, 1].wait_recv()
 
-        def keep(t, z):
+        def keep(r, z):
             if stage == 3:
-                near[1, k, :, pl.ds(t * tile, tile)] = z
+                near[1, k, :, r] = z
             else:
-                close(k, t, z)
+                close(k, r, z)
         pull(wg if stage == 3 else part, k, pl.ds(slab, 3 * slab), keep)
 
     def finish(stage, k):
@@ -296,12 +295,9 @@
             for c_ in cp.values():
                 c_.wait_send()
         elif stage == 3:
-            def keep(t, z):
-                at = pl.ds(t * tile, tile)
-                near[1, k, :, at] = near[1, k, :, at] + z
-                if t == 1:
-                    z_copies[k].start()
-            pull(wg, k, FAR, keep)
+            def keep(r, z):
+                near[1, k, :, r] = near[1, k, :, r] + z
+            pull(wg, k, FAR, keep, z_copies[k].start)
             z_copies[k].wait_recv()
 
             def second_weights(i):
@@ -315,29 +311,37 @@
         else:
             pull(part, k, FAR, functools.partial(close, k))
 
-    loads[0, 0].wait()
-    loads[0, 1].wait()
-    pl.semaphore_wait(barrier, 3 + planes - 1)
+    def other(k, i):
+        if k == 0:
+            loads[0, i].wait()
+        select_other(k, i)
+        if (k, i) == (0, 0):
+            pl.semaphore_wait(barrier, 3 + 2 * (planes - 1))
+        m_copies[k, i].start()
+
+    def own(k, i):
+        if k == 0:
+            loads[1, i].wait()
+        select_own(k, i)
+
     for k in range(CHUNKS):
-        select_other(k, 0)
-    loads[1, 0].wait()
-    loads[1, 1].wait()
+        for i in range(3):
+            other(k, i)
+        own(k, 0)
+        copies[0, k][TO_P, 0].start()
+        copies[0, k][TO_Q, 0].start()
+        own(k, 1)
+        copies[0, k][TO_P, 1].start()
+        own(k, 2)
+        copies[0, k][TO_Q, 1].start()
     for k in range(CHUNKS):
-        select_own(k, 0)
-        send_first(0, k)
-    loads[0, 2].wait()
-    loads[0, 3].wait()
-    for k in range(CHUNKS):
-        select_other(k, 1)
+        other(k, 3)
     for copy in a_copies:
         copy.start()
-    loads[1, 2].wait()
-    loads[1, 3].wait()
+    middle(0, 0)
     for k in range(CHUNKS):
-        select_own(k, 1)
-        copies[0, k][TO_Q, 1].start()
-    for k in range(CHUNKS):
-        middle(0, k)
+        own(k, 3)
+    middle(0, 1)
     for stage in range(1, 5):
         finish(stage - 1, 0)
         start(stage, 0)
@@ -353,24 +357,29 @@
     nears(4, 1)
     finish(4, 1)
 
-    bc_send[...] = bc[:, mate_half]
-    bc_copy.start()
-    bc_copy.wait_recv()
-    plane[pl.ds(s_me, 1)] = ((bc[:, own_half] + bc_recv[...]) * scale)[None]
+    total[...] = bc[...] * scale
+    plane[0, pl.ds(s_me, 1)] = total[:, own_half][None]
     plane_copies = []
-    for o in range(1, planes):
-        copy = pltpu.make_async_remote_copy(src_ref=plane.at[s_me], dst_ref=plane.at[s_me], send_sem=plane_s.at[o],
-                                            recv_sem=plane_r.at[o],
-                                            device_id={"src": lax.rem(s_me + o, planes)}, device_id_type=MESH)
-        copy.start()
-        plane_copies.append(copy)
-    for o in range(1, planes):
-        arrived = plane.at[lax.rem(s_me + planes - o, planes)]
-        pltpu.make_async_remote_copy(src_ref=arrived, dst_ref=arrived, send_sem=plane_s.at[o], recv_sem=plane_r.at[o],
-                                     device_id={"src": lax.rem(s_me + o, planes)}, device_id_type=MESH).wait_recv()
-    out[...] = jnp.sum(plane[...], axis=0)
-
-    for copy in plane_copies + a_copies + x1_copies + x2_copies + z_copies + [bc_copy]:
+    for o in range(planes):
+        there = lax.rem(s_me + o, planes)
+        back = lax.rem(s_me + planes - o, planes)
+        for other_core in (0, 1):
+            if o == 0 and not other_core:
+                continue
+            device = {"src": there, "graph": x * 2 + (1 - c)} if other_core else {"src": there}
+
+            def plane_copy(target):
+                return pltpu.make_async_remote_copy(src_ref=total.at[:, side[other_core]], dst_ref=plane.at[other_core, target],
+                                                    send_sem=plane_s.at[other_core * planes + o],
+                                                    recv_sem=plane_r.at[other_core * planes + o],
+                                                    device_id=device, device_id_type=MESH)
+            plane_copy(s_me).start()
+            plane_copies.append(plane_copy(back))
+    for copy in plane_copies:
+        copy.wait_recv()
+    out[...] = jnp.sum(plane[0], axis=0) + jnp.sum(plane[1], axis=0)
+
+    for copy in plane_copies + a_copies + x1_copies + x2_copies + z_copies:
         copy.wait_send()
     for k in range(CHUNKS):
         for stage in (3, 4):
@@ -390,7 +399,7 @@
         wide = 4 * slab
         vmem = pltpu.VMEM
         sem = pltpu.SemaphoreType.DMA
-        mates = 5 + 5 * CHUNKS
+        mates = 4 + 7 * CHUNKS
         rings = 5 * CHUNKS * 6
         flops = 2 * 9 * src_count * slab * vertex_count
         bc = pl.pallas_call(
@@ -405,8 +414,8 @@
                 vmem((CHUNKS, m, wide), f32), vmem((CHUNKS, m, wide), f32),
                 vmem((CHUNKS, m, 2 * slab), bf16), vmem((CHUNKS, 2, m // 2, slab), bf16),
                 vmem((2, CHUNKS, m, 2 * slab), f32), vmem((2, CHUNKS, 2, m // 2, slab), f32),
-                vmem((1, 2 * slab), f32), vmem((1, slab), f32), vmem((1, slab), f32), vmem((planes, 1, slab), f32),
-                sem((8,)), sem((rings,)), sem((rings,)), sem((mates,)), sem((mates,)), sem((planes,)), sem((planes,)),
+                vmem((1, 2 * slab), f32), vmem((1, 2 * slab), f32), vmem((2, planes, 1, slab), f32),
+                sem((8,)), sem((rings,)), sem((rings,)), sem((mates,)), sem((mates,)), sem((2 * planes,)), sem((2 * planes,)),
             ],
             compiler_params=pltpu.CompilerParams(collective_id=0, has_side_effects=True, vmem_limit_bytes=67043328),
             cost_estimate=pl.CostEstimate(flops=flops, bytes_accessed=2 * slab * vertex_count, transcendentals=0),

time: 205 us -> 206 us (level)
  no operation moved by 1% of the time
where the time goes in v3:
time: 206 us
  Pallas kernels  205 us (100%)
    pallas_call x1, Pallas kernels, device_program(): pl.pallas_call(functools.partial(kernel, ring, planes, scale), out_shape=...  205 us

profile of v3, /device:TPU:1, one launch (start us, length us, event | category | flops | bytes accessed | tf_op | source)
XLA Modules:
  0.0 205.9 jit_solution(8535800126975261613)
XLA Ops:
  0.0 204.6 %shard_map.37 = f32[1,1152]{1,0:T(1,128)} custom-call(bf16[1152,9216]{1,0:T(8,128)(2,1)} %adj.1, s32[1,256]{1,0:T(1,128)} %bitcast.1, f32[2]{0:T(128)} %lw.1), custom_call_target="tpu_custom_call" | custom-call | flops 48922361856 | bytes 21233664 | tf_op jit(solution)/shard_map/pallas_call | solution.py:405
  204.6 1.3 reduce
